TPU v7x, 32 devices: a whole 2x2x4 slice. The times are simulated.
32 devices in a mesh: job: 4 (over y, x), dp: 2 (over core), tp: 4 (over z).
Axes of the slice: x: 2, y: 2, z: 4, core: 2. Of those that a mesh axis runs over, the one named last changes fastest.
Arguments:
- partial_up: float32 [8, 768, 3072], P(('job', 'dp'), None, 'tp'), parts along dimension 0, may hold values from -0.875 to 0.875
- partial_down: float32 [8, 3072, 768], P(('job', 'dp'), 'tp'), parts along dimension 0, may hold values from -0.875 to 0.875
- partial_norm: float32 [8, 768], P(('job', 'dp')), parts along dimension 0, may hold values from -8 to 8
- partial_bias: float32 [8, 768], P(('job', 'dp')), parts along dimension 0, may hold values from -8 to 8
- master_up: float32 [3072, 3072], P(('job', 'dp'), 'tp'), parts along dimension 0, may hold values from -0.3125 to 0.3125
- master_down: float32 [12288, 768], P(('job', 'tp'), 'dp'), parts along dimension 0, may hold values from -0.15625 to 0.15625
- master_norm: float32 [3072], P(('job', 'dp')), parts along dimension 0, may hold values from 0.25 to 1.75
- master_bias: float32 [3072], P(('job', 'dp')), parts along dimension 0, may hold values from -3 to 3
- memory_up: float32 [3072, 3072], P(('job', 'dp'), 'tp'), parts along dimension 0, may hold values from -0.21875 to 0.21875
- memory_down: float32 [12288, 768], P(('job', 'tp'), 'dp'), parts along dimension 0, may hold values from -0.109375 to 0.109375
- memory_norm: float32 [3072], P(('job', 'dp')), parts along dimension 0, may hold values from -1.75 to 1.75
- memory_bias: float32 [3072], P(('job', 'dp')), parts along dimension 0, may hold values from -1.75 to 1.75
Outputs:
- compute_up: bfloat16 [3072, 3072], P('job', 'tp'), parts along dimension 0
- compute_down: bfloat16 [12288, 768], P(('job', 'tp')), parts along dimension 0
- compute_norm: bfloat16 [3072], P('job'), parts along dimension 0
- compute_bias: bfloat16 [3072], P('job'), parts along dimension 0
- stepped_up: float32 [3072, 3072], P(('job', 'dp'), 'tp'), parts along dimension 0
- stepped_down: float32 [12288, 768], P(('job', 'tp'), 'dp'), parts along dimension 0
- stepped_norm: float32 [3072], P(('job', 'dp')), parts along dimension 0
- stepped_bias: float32 [3072], P(('job', 'dp')), parts along dimension 0
- state_new_up: float32 [3072, 3072], P(('job', 'dp'), 'tp'), parts along dimension 0
- state_new_down: float32 [12288, 768], P(('job', 'tp'), 'dp'), parts along dimension 0
- state_new_norm: float32 [3072], P(('job', 'dp')), parts along dimension 0
- state_new_bias: float32 [3072], P(('job', 'dp')), parts along dimension 0
There are 4 independent parts, one for each index of `job`. A program takes and returns all parts, laid end to end along the dimension named above; each array names one. Nothing has to cross between parts.
All inputs are finite; a program needn't handle non-finite values.
Results may differ from a plain program's by a relative error of at most 0.001.
Values may be sent and summed in bfloat16 or wider, within the bound.
A program may use at most 64 MiB of HBM per device.

v0:
```python
import jax
import jax.numpy as jnp
from jax import lax
from jax.sharding import PartitionSpec as P

learn_rate = 0.4
hold_rate = 0.9


def on_device(
    partial_up,
    partial_down,
    partial_norm,
    partial_bias,
    master_up,
    master_down,
    master_norm,
    master_bias,
    memory_up,
    memory_down,
    memory_norm,
    memory_bias,
):
    mean_up, mean_down = (
        lax.psum_scatter(partial_up[0], "dp", scatter_dimension=0, tiled=True),
        lax.psum_scatter(partial_down[0], "dp", scatter_dimension=1, tiled=True),
    )
    whole_norm, whole_bias = lax.psum((partial_norm[0], partial_bias[0]), "dp")
    place = lax.axis_index("dp")
    mean_norm = lax.dynamic_slice_in_dim(
        whole_norm, place * master_norm.shape[0], master_norm.shape[0]
    )
    mean_bias = lax.dynamic_slice_in_dim(
        whole_bias, place * master_bias.shape[0], master_bias.shape[0]
    )
    mean_rate = lax.axis_size("dp") ** (-0.5)
    mean_up = mean_up * mean_rate
    mean_down = mean_down * mean_rate
    mean_norm = mean_norm * mean_rate
    mean_bias = mean_bias * mean_rate
    own_up, own_down, slope_up_norm, slope_down_norm = lax.psum(
        (
            jnp.sum(master_up * master_up, axis=1, keepdims=True),
            jnp.sum(master_down * master_down, axis=0, keepdims=True),
            jnp.sum(mean_up * mean_up, axis=1, keepdims=True),
            jnp.sum(mean_down * mean_down, axis=0, keepdims=True),
        ),
        "tp",
    )
    mean_up = mean_up * (jnp.sqrt(own_up) * lax.rsqrt(slope_up_norm + 1e-06))
    mean_down = mean_down * (jnp.sqrt(own_down) * lax.rsqrt(slope_down_norm + 1e-06))
    state_new_up = hold_rate * memory_up + mean_up
    stepped_up = master_up - learn_rate * state_new_up
    state_new_down = hold_rate * memory_down + mean_down
    stepped_down = master_down - learn_rate * state_new_down
    state_new_norm = hold_rate * memory_norm + mean_norm
    stepped_norm = master_norm - learn_rate * state_new_norm
    state_new_bias = hold_rate * memory_bias + mean_bias
    stepped_bias = master_bias - learn_rate * state_new_bias
    compute_up, compute_down, compute_norm, compute_bias = (
        lax.all_gather(stepped_up.astype(jnp.bfloat16), "dp", axis=0, tiled=True),
        lax.all_gather(stepped_down.astype(jnp.bfloat16), "dp", axis=1, tiled=True),
        lax.all_gather(stepped_norm.astype(jnp.bfloat16), "dp", axis=0, tiled=True),
        lax.all_gather(stepped_bias.astype(jnp.bfloat16), "dp", axis=0, tiled=True),
    )
    return (
        compute_up,
        compute_down,
        compute_norm,
        compute_bias,
        stepped_up,
        stepped_down,
        stepped_norm,
        stepped_bias,
        state_new_up,
        state_new_down,
        state_new_norm,
        state_new_bias,
    )


def solution(mesh):
    in_specs = (
        P(("job", "dp"), None, "tp"),
        P(("job", "dp"), "tp", None),
        P(("job", "dp"), None),
        P(("job", "dp"), None),
        P(("job", "dp"), "tp"),
        P(("job", "tp"), "dp"),
        P(("job", "dp")),
        P(("job", "dp")),
        P(("job", "dp"), "tp"),
        P(("job", "tp"), "dp"),
        P(("job", "dp")),
        P(("job", "dp")),
    )
    out_specs = (
        P("job", "tp"),
        P(("job", "tp"), None),
        P("job"),
        P("job"),
        P(("job", "dp"), "tp"),
        P(("job", "tp"), "dp"),
        P(("job", "dp")),
        P(("job", "dp")),
        P(("job", "dp"), "tp"),
        P(("job", "tp"), "dp"),
        P(("job", "dp")),
        P(("job", "dp")),
    )
    return jax.shard_map(
        on_device, mesh=mesh, in_specs=in_specs, out_specs=out_specs, check_vma=False
    )
```

profile of v0, /device:TPU:0, one launch (start us, length us, event | category | flops | bytes accessed | tf_op | source)
XLA Modules:
  0.0 83.8 jit_solution(7850769478570783003)
XLA Ops:
  7.2 0.0 reduce-scatter.3.cloned.1.call-start
  7.2 0.7 reduce-scatter.3.cloned.1.call-update
  7.9 0.0 reduce-scatter.5.cloned.1.call-start
  8.0 0.7 reduce-scatter.5.cloned.1.call-update
  8.7 0.0 all-gather.7.cloned.1.call-start
  8.7 0.5 copy-done.1
  9.2 0.2 multiply_reduce_fusion.3
  9.4 0.6 copy-done
  10.0 0.1 multiply_reduce_fusion.1
  10.2 12.9 %reduce-scatter.3.cloned.1.call-done = f32[384,768]{1,0:T(8,128)} async-done(((f32[768,768]{1,0:T(8,128)}), f32[384,768]{1,0:T(8,128)}) %reduce-scatter.3.cloned.1.call-update) | async-done | bytes 1179664 | tf_op jit(solution)/shard_map/reduce_scatter | solution.py:25
  23.1 1.5 %multiply_reduce_fusion.2 = f32[384]{0:T(512)S(1)} fusion(f32[384,768]{1,0:T(8,128)} %reduce-scatter.3.cloned.1.call-done), kind=kLoop, calls=%fused_computation.6 | loop fusion | flops 884352 | bytes 1181184 | tf_op jit(solution)/shard_map/reduce_sum | solution.py:45
  24.6 12.1 %reduce-scatter.5.cloned.1.call-done = f32[768,384]{1,0:T(8,128)} async-done(((f32[768,768]{1,0:T(8,128)}), f32[768,384]{1,0:T(8,128)}) %reduce-scatter.5.cloned.1.call-update) | async-done | bytes 1179664 | tf_op jit(solution)/shard_map/reduce_scatter | solution.py:26
  36.6 1.4 %multiply_reduce_fusion = f32[384]{0:T(512)S(1)} fusion(f32[768,384]{1,0:T(8,128)} %reduce-scatter.5.cloned.1.call-done), kind=kLoop, calls=%fused_computation.2 | loop fusion | flops 884352 | bytes 1181184 | tf_op jit(solution)/shard_map/reduce_sum | solution.py:46
  38.1 12.2 %all-reduce = (f32[384,1]{0,1:T(1,128)S(1)}, f32[384,1]{0,1:T(1,128)S(1)}, f32[1,384]{1,0:T(1,128)S(1)}, f32[1,384]{1,0:T(1,128)S(1)}) all-reduce(f32[384,1]{0,1:T(1,128)S(1)} %broadcast_in_dim.13, f32[384,1]{0,1:T(1,128)S(1)} %broadcast_in_dim.12, f32[1,384]{1,0:T(1,128)S(1)} %broadcast_in_dim.15, ...), channel_id=1, replica_groups=mesh['job'=4,'dp'=2,'tp'=4] {'tp'}, use_global_device_ids=true, to_apply=%region_4.0 | all-reduce | flops 1536 | bytes 12288 | tf_op jit(solution)/shard_map/psum | solution.py:41
  50.3 3.6 %fusion.2 = (bf16[768,384]{1,0:T(8,128)(2,1)}, f32[768,384]{1,0:T(8,128)}, f32[768,384]{1,0:T(8,128)}) fusion(f32[768,384]{1,0:T(8,128)S(1)} %copy-done, f32[768,384]{1,0:T(8,128)} %reduce-scatter.5.cloned.1.call-done, f32[384]{0:T(512)S(1)} %multiply_reduce_fusion.4, f32[768,384]{1,0:T(8,128)} %param.21), kind=kLoop, calls=%fused_computation.16 | loop fusion | flops 1769472 | bytes 6489600 | tf_op jit(solution)/shard_map/convert_element_type | solution.py:62
  53.8 0.0 all-gather.7.cloned.1.call-update
  53.9 0.0 all-gather.5.cloned.1.call-start
  54.0 0.0 copy-start.4
  54.0 0.0 copy-start.5
  54.0 0.0 copy-start.8
  54.0 3.2 %fusion.3 = (bf16[384,768]{1,0:T(8,128)(2,1)}, f32[384,768]{1,0:T(8,128)}, f32[384,768]{1,0:T(8,128)}) fusion(f32[384,768]{1,0:T(8,128)S(1)} %copy-done.1, f32[384,768]{1,0:T(8,128)S(1)} %copy-done.2, f32[384]{0:T(512)S(1)} %multiply_reduce_fusion.5, f32[384,768]{1,0:T(8,128)} %param.20), kind=kLoop, calls=%fused_computation.17 | loop fusion | flops 1769472 | bytes 6489600 | tf_op jit(solution)/shard_map/convert_element_type | solution.py:61
  57.2 0.0 all-gather.5.cloned.1.call-update
  57.3 2.5 %all-reduce.1 = (f32[768]{0:T(1024)S(1)}, f32[768]{0:T(1024)S(1)}) all-reduce(f32[768]{0:T(1024)S(1)} %reduce.2, f32[768]{0:T(1024)S(1)} %reduce.4), channel_id=1, replica_groups=mesh['job'=4,'dp'=2,'tp'=4] {'dp'}, use_global_device_ids=true, to_apply=%region_10.0 | all-reduce | flops 1536 | bytes 12288 | tf_op jit(solution)/shard_map/psum | solution.py:28
  59.8 0.7 fusion.1
  60.5 1.8 %all-gather = bf16[2,1,384]{2,1,0:T(2,128)(2,1)S(1)} all-gather(bf16[1,1,384]{2,1,0:T(2,128)(2,1)S(1)} %reshape.28), channel_id=1, replica_groups=mesh['job'=4,'dp'=2,'tp'=4] {'dp'}, dimensions={0}, use_global_device_ids=true | all-gather | bytes 2304 | tf_op jit(solution)/shard_map/all_gather | solution.py:63
  62.3 0.6 reshape.29
  62.9 0.7 fusion
  63.6 1.8 %all-gather.1 = bf16[2,1,384]{2,1,0:T(2,128)(2,1)S(1)} all-gather(bf16[1,1,384]{2,1,0:T(2,128)(2,1)S(1)} %reshape.30), channel_id=1, replica_groups=mesh['job'=4,'dp'=2,'tp'=4] {'dp'}, dimensions={0}, use_global_device_ids=true | all-gather | bytes 2304 | tf_op jit(solution)/shard_map/all_gather | solution.py:64
  65.4 0.6 reshape.31
  66.0 7.7 %all-gather.5.cloned.1.call-done = bf16[768,768]{1,0:T(8,128)(2,1)} async-done(((bf16[384,768]{1,0:T(8,128)(2,1)}), bf16[768,768]{1,0:T(8,128)(2,1)}) %all-gather.5.cloned.1.call-update) | async-done | bytes 1179664 | tf_op jit(solution)/shard_map/all_gather | solution.py:61
  73.8 2.5 %copy.26 = bf16[768,768]{1,0:T(8,128)(2,1)} copy(bf16[768,768]{1,0:T(8,128)(2,1)} %all-gather.5.cloned.1.call-done) | data formatting | bytes 2359296
  76.2 1.0 %copy.27 = bf16[768,768]{1,0:T(8,128)(2,1)} copy(bf16[768,768]{1,0:T(8,128)(2,1)S(1)} %copy-done.3) | data formatting | bytes 2359296
  (28 shorter events, 0.2 us)
Async XLA Ops:
  7.2 15.9 %reduce-scatter.3.cloned.1.call-start = ((), (), s32[]{:S(2)}) async-start(), calls=%async_computation.2 | async-start | bytes 3538944 | tf_op jit(solution)/shard_map/reduce_scatter | solution.py:25
  7.9 28.7 %reduce-scatter.5.cloned.1.call-start = ((), (), s32[]{:S(2)}) async-start(), calls=%async_computation.4 | async-start | bytes 3538944 | tf_op jit(solution)/shard_map/reduce_scatter | solution.py:26
  8.0 1.3 %copy-start.1 = (f32[384,768]{1,0:T(8,128)S(1)}, f32[384,768]{1,0:T(8,128)}, u32[]{:S(2)}) copy-start(f32[384,768]{1,0:T(8,128)} %param.16) | copy-start | bytes 3538948
  8.7 1.4 %copy-start = (f32[768,384]{1,0:T(8,128)S(1)}, f32[768,384]{1,0:T(8,128)}, u32[]{:S(2)}) copy-start(f32[768,384]{1,0:T(8,128)} %param.17) | copy-start | bytes 3538948
  8.7 57.4 %all-gather.7.cloned.1.call-start = ((), (), s32[]{:S(2)}) async-start(), calls=%async_computation.5 | async-start | bytes 1769472 | tf_op jit(solution)/shard_map/all_gather | solution.py:62
  50.3 3.7 %copy-start.2 = (f32[384,768]{1,0:T(8,128)S(1)}, f32[384,768]{1,0:T(8,128)}, u32[]{:S(2)}) copy-start(f32[384,768]{1,0:T(8,128)} %reduce-scatter.3.cloned.1.call-done) | copy-start | bytes 3538948
  53.9 19.9 %all-gather.5.cloned.1.call-start = ((), (), s32[]{:S(2)}) async-start(), calls=%async_computation.3 | async-start | bytes 1769472 | tf_op jit(solution)/shard_map/all_gather | solution.py:61
  54.0 3.3 %copy-start.4 = (f32[1,768]{1,0:T(1,128)S(1)}, f32[1,768]{1,0:T(1,128)}, u32[]{:S(2)}) copy-start(f32[1,768]{1,0:T(1,128)} %param.14) | copy-start | bytes 9220
  54.0 3.3 %copy-start.5 = (f32[1,768]{1,0:T(1,128)S(1)}, f32[1,768]{1,0:T(1,128)}, u32[]{:S(2)}) copy-start(f32[1,768]{1,0:T(1,128)} %param.15) | copy-start | bytes 9220
  54.0 5.8 %copy-start.6 = (f32[384]{0:T(512)S(1)}, f32[384]{0:T(512)}, u32[]{:S(2)}) copy-start(f32[384]{0:T(512)} %param.18) | copy-start | bytes 4612
  54.0 5.8 %copy-start.7 = (f32[384]{0:T(512)S(1)}, f32[384]{0:T(512)}, u32[]{:S(2)}) copy-start(f32[384]{0:T(512)} %param.22) | copy-start | bytes 4612
  54.0 8.9 %copy-start.8 = (f32[384]{0:T(512)S(1)}, f32[384]{0:T(512)}, u32[]{:S(2)}) copy-start(f32[384]{0:T(512)} %param.19) | copy-start | bytes 4612
  54.0 8.9 %copy-start.9 = (f32[384]{0:T(512)S(1)}, f32[384]{0:T(512)}, u32[]{:S(2)}) copy-start(f32[384]{0:T(512)} %param.23) | copy-start | bytes 4612
  73.8 2.5 %copy-start.3 = (bf16[768,768]{1,0:T(8,128)(2,1)S(1)}, bf16[768,768]{1,0:T(8,128)(2,1)}, u32[]{:S(2)}) copy-start(bf16[768,768]{1,0:T(8,128)(2,1)} %all-gather.7.cloned.1.call-done) | copy-start | bytes 3538948
Sparse Core Ops, SparseCore 0:
  10.2 12.8 reduce-scatter.2
  25.3 11.2 reduce-scatter.4
  54.0 7.3 all-gather.6
  63.3 10.3 all-gather.4
where the time goes:
time: 84.1 us; the launch traced here: 83.8 us
  waiting for transfers between devices  34.1 us (41%)
  blocking collectives  18.3 us (22%)
  between operations  13.9 us (17%)
  other arithmetic  11.4 us (14%)
  local copies, waits for them, and re-layouts  5.88 us (7%)
    reduce_scatter x1, waiting for transfers between devices, on_device(): lax.psum_scatter(partial_up[0], 'dp', scatter_dimension=0, tiled=True)  12.9 us
    psum x1, blocking collectives, on_device(): lax.psum((jnp.sum(master_up * master_up, axis=1, keepdims=True), jnp.sum(...  12.2 us
    reduce_scatter x1, waiting for transfers between devices, on_device(): lax.psum_scatter(partial_down[0], 'dp', scatter_dimension=1, tiled=True)  12.1 us
    all_gather x1, waiting for transfers between devices, on_device(): lax.all_gather(stepped_up.astype(jnp.bfloat16), 'dp', axis=0, tiled=True)  7.73 us
    unnamed x26, local copies, waits for them, and re-layouts  5.86 us
    convert_element_type x1, other arithmetic, on_device(): stepped_down.astype(jnp.bfloat16)  3.57 us
    convert_element_type x1, other arithmetic, on_device(): stepped_up.astype(jnp.bfloat16)  3.19 us
    psum x1, blocking collectives, on_device(): whole_norm, whole_bias = lax.psum((partial_norm[0], partial_bias[0]), 'dp')  2.5 us
  transfers between devices with their start and end apart: 4, of which 3 were waited for; matrix products, arithmetic and copies ran while one was open for 9% of the time, Pallas kernels for 0%

commit v1 on v0

--- a/solution.py
+++ b/solution.py
@@ -1,6 +1,10 @@
+import functools
+
 import jax
 import jax.numpy as jnp
 from jax import lax
+from jax.experimental import pallas as pl
+from jax.experimental.pallas import tpu as pltpu
 from jax.sharding import PartitionSpec as P
 
 learn_rate = 0.4
@@ -79,6 +83,326 @@
     )
 
 
+chunks = 4
+lanes = 128
+
+
+def lane_sums(x):
+    total = x[:, :lanes]
+    for at in range(lanes, x.shape[1], lanes):
+        total = total + x[:, at : at + lanes]
+    return total
+
+
+def exchange(
+    pu, pd, pn, pb, mu_h, md_h, mn, mb, eu_h, ed_h, en, eb,
+    cu, cd, cn, cb, su, sd, sn, sb, tu, td, tn, tb,
+    own_u, own_d, got_u, got_d, mu, md, eu, ed, vec, got_vec,
+    sq_u, acc_d, stat_u, stat_d,
+    load_sem, part_send, part_recv, vec_sem, stat_send, stat_recv, out_send, out_recv,
+):
+    me = lax.axis_index("dp")
+    peer = 1 - me
+    here = lax.axis_index("tp")
+    n = lax.axis_size("tp")
+    rate = lax.axis_size("dp") ** (-0.5)
+    rows, wide = mu.shape
+    tall, cols = md.shape
+    part_u, part_d = rows // chunks, tall // chunks
+
+    def mine(size):
+        return pl.ds(pl.multiple_of(me * size, size), size)
+
+    def theirs(size):
+        return pl.ds(pl.multiple_of(peer * size, size), size)
+
+    barrier = pltpu.get_barrier_semaphore()
+    pl.semaphore_signal(barrier, inc=1, device_id={"dp": peer})
+    for step in range(1, n):
+        pl.semaphore_signal(barrier, inc=1, device_id={"tp": lax.rem(here + step, n)})
+
+    loads = [
+        pltpu.make_async_copy(source, target, load_sem.at[at])
+        for at, (source, target) in enumerate((
+            (mu_h, mu),
+            (md_h, md),
+            (pu.at[mine(rows), :], own_u),
+            (pd.at[:, mine(cols)], own_d),
+            (eu_h, eu),
+            (ed_h, ed),
+        ))
+    ]
+    for load in loads:
+        load.start()
+
+    half = mn.shape[-1]
+    vec[0:1, :] = pn[...]
+    vec[1:2, :] = pb[...]
+    vec[2:3, :half] = mn[...].reshape(1, half)
+    vec[2:3, half:] = en[...].reshape(1, half)
+    vec[3:4, :half] = mb[...].reshape(1, half)
+    vec[3:4, half:] = eb[...].reshape(1, half)
+
+    pl.semaphore_wait(barrier, n)
+
+    send_u, send_d = [], []
+    for at in range(chunks):
+        span = pl.ds(at * part_u, part_u)
+        send_u.append(pltpu.make_async_remote_copy(
+            src_ref=pu.at[pl.ds(pl.multiple_of(peer * rows + at * part_u, 8), part_u), :],
+            dst_ref=got_u.at[span, :],
+            send_sem=part_send.at[0, at],
+            recv_sem=part_recv.at[0, at],
+            device_id={"dp": peer},
+        ))
+        span = pl.ds(at * part_d, part_d)
+        send_d.append(pltpu.make_async_remote_copy(
+            src_ref=pd.at[span, theirs(cols)],
+            dst_ref=got_d.at[span, :],
+            send_sem=part_send.at[1, at],
+            recv_sem=part_recv.at[1, at],
+            device_id={"dp": peer},
+        ))
+    for copy in send_u + send_d:
+        copy.start()
+    send_vec = pltpu.make_async_remote_copy(
+        src_ref=vec, dst_ref=got_vec, send_sem=vec_sem.at[0], recv_sem=vec_sem.at[1],
+        device_id={"dp": peer},
+    )
+    send_vec.start()
+
+    step_u, step_d = 32, 64
+
+    loads[0].wait()
+
+    @pl.loop(0, rows // step_u)
+    def _(at):
+        span = pl.ds(pl.multiple_of(at * step_u, step_u), step_u)
+        x = mu[span, :]
+        sq_u[span, :] = lane_sums(x * x)
+
+    stat_u[pl.ds(here, 1), 0:1, :] = jnp.sum(sq_u[...].T, axis=0).reshape(1, 1, rows)
+
+    def down_squares(read, start, count):
+        @pl.loop(0, count // step_d)
+        def _(at):
+            span = pl.ds(pl.multiple_of(start + at * step_d, step_d), step_d)
+            x = read(span)
+            acc_d[...] += jnp.sum((x * x).reshape(step_d // 8, 8, cols), axis=0)
+
+    loads[1].wait()
+    acc_d[...] = jnp.zeros_like(acc_d)
+    down_squares(lambda span: md[span, :], 0, tall)
+    stat_d[pl.ds(here, 1), 0:1, :] = jnp.sum(acc_d[...], axis=0).reshape(1, 1, cols)
+    acc_d[...] = jnp.zeros_like(acc_d)
+
+    def to_peers(stat, which):
+        copies = []
+        for step in range(1, n):
+            copies.append(pltpu.make_async_remote_copy(
+                src_ref=stat.at[here],
+                dst_ref=stat.at[here],
+                send_sem=stat_send.at[which, step - 1],
+                recv_sem=stat_recv.at[which, step - 1],
+                device_id={"tp": lax.rem(here + step, n)},
+            ))
+        for copy in copies:
+            copy.start()
+        return copies
+
+    loads[2].wait()
+    for chunk in range(chunks):
+        send_u[chunk].wait_recv()
+
+        @pl.loop(0, part_u // step_u)
+        def _(at):
+            span = pl.ds(pl.multiple_of(chunk * part_u + at * step_u, step_u), step_u)
+            x = (own_u[span, :] + got_u[span, :]) * rate
+            own_u[span, :] = x
+            sq_u[span, :] = lane_sums(x * x)
+
+    stat_u[pl.ds(here, 1), 1:2, :] = jnp.sum(sq_u[...].T, axis=0).reshape(1, 1, rows)
+    stats_u = to_peers(stat_u, 0)
+
+    loads[3].wait()
+
+    def summed(span):
+        x = (own_d[span, :] + got_d[span, :]) * rate
+        own_d[span, :] = x
+        return x
+
+    for chunk in range(chunks):
+        send_d[chunk].wait_recv()
+        down_squares(summed, chunk * part_d, part_d)
+    stat_d[pl.ds(here, 1), 1:2, :] = jnp.sum(acc_d[...], axis=0).reshape(1, 1, cols)
+    stats_d = to_peers(stat_d, 1)
+
+    send_vec.wait()
+    mean = (vec[0:2, :] + got_vec[0:2, :]) * rate
+    for at, (state, stepped, rounded) in enumerate(((tn, sn, cn), (tb, sb, cb))):
+        row = slice(2 + at, 3 + at)
+        low, high = mean[at : at + 1, :half], mean[at : at + 1, half:]
+        new_own = hold_rate * vec[row, half:] + jnp.where(me == 0, low, high)
+        own = vec[row, :half] - learn_rate * new_own
+        new_other = hold_rate * got_vec[row, half:] + jnp.where(me == 0, high, low)
+        other = got_vec[row, :half] - learn_rate * new_other
+        state[...] = new_own.reshape(state.shape)
+        stepped[...] = own.reshape(stepped.shape)
+        whole = jnp.concatenate(
+            [jnp.where(me == 0, own, other), jnp.where(me == 0, other, own)], axis=1
+        )
+        rounded[...] = whole.reshape(rounded.shape).astype(rounded.dtype)
+
+    def ratio_of(stat):
+        total = stat[0]
+        for at in range(1, n):
+            total = total + stat[at]
+        return jnp.sqrt(total[0:1, :]) * lax.rsqrt(total[1:2, :] + 1e-06)
+
+    loads[4].wait()
+    for copy in stats_u:
+        copy.wait()
+    sq_u[...] = jnp.broadcast_to(ratio_of(stat_u), (lanes, rows)).T
+
+    out = []
+    pieces = 2
+    for piece in range(pieces):
+        size = rows // pieces
+
+        @pl.loop(0, size // step_u)
+        def _(at):
+            start = piece * size + at * step_u
+            span = pl.ds(pl.multiple_of(start, step_u), step_u)
+            ratio = sq_u[span, :]
+            ratio = jnp.concatenate([ratio] * (wide // lanes), axis=1)
+            state = hold_rate * eu[span, :] + own_u[span, :] * ratio
+            stepped = mu[span, :] - learn_rate * state
+            tu[span, :] = state
+            su[span, :] = stepped
+            place = pl.ds(pl.multiple_of(me * rows + start, step_u), step_u)
+            cu[place, :] = stepped.astype(cu.dtype)
+
+        span = pl.ds(pl.multiple_of(me * rows + piece * size, step_u), size)
+        out.append(pltpu.make_async_remote_copy(
+            src_ref=cu.at[span, :],
+            dst_ref=cu.at[span, :],
+            send_sem=out_send.at[0, piece],
+            recv_sem=out_recv.at[0, piece],
+            device_id={"dp": peer},
+        ))
+        out[-1].start()
+
+    loads[5].wait()
+    for copy in stats_d:
+        copy.wait()
+    ratio_d = ratio_of(stat_d)
+    acc_d[...] = jnp.broadcast_to(ratio_d, acc_d.shape)
+    for piece in range(pieces):
+        size = tall // pieces
+
+        @pl.loop(0, size // step_d)
+        def _(at):
+            span = pl.ds(pl.multiple_of(piece * size + at * step_d, step_d), step_d)
+            ratio = jnp.broadcast_to(acc_d[...][None], (step_d // 8, 8, cols)).reshape(step_d, cols)
+            state = hold_rate * ed[span, :] + own_d[span, :] * ratio
+            stepped = md[span, :] - learn_rate * state
+            td[span, :] = state
+            sd[span, :] = stepped
+            cd[span, mine(cols)] = stepped.astype(cd.dtype)
+
+        span = pl.ds(piece * size, size)
+        out.append(pltpu.make_async_remote_copy(
+            src_ref=cd.at[span, mine(cols)],
+            dst_ref=cd.at[span, mine(cols)],
+            send_sem=out_send.at[1, piece],
+            recv_sem=out_recv.at[1, piece],
+            device_id={"dp": peer},
+        ))
+        out[-1].start()
+
+    for copy in send_u + send_d:
+        copy.wait_send()
+    for copy in out:
+        copy.wait()
+
+
+def place_results(*refs):
+    count = (len(refs) - 1) // 2
+    sem = refs[-1]
+    copies = [
+        pltpu.make_async_copy(refs[at], refs[count + at], sem.at[at]) for at in range(count)
+    ]
+    for copy in copies:
+        copy.start()
+    for copy in copies:
+        copy.wait()
+
+
+def held(arrays):
+    return [pltpu.with_memory_space_constraint(x, pltpu.HBM) for x in arrays]
+
+
+def on_pair(*args):
+    pu, pd, pn, pb, mu, md, mn, mb, eu, ed, en, eb = args
+    n = lax.axis_size("tp")
+    f32, bf16 = jnp.float32, jnp.bfloat16
+    vmem = pl.BlockSpec(memory_space=pltpu.VMEM)
+    hbm = pl.BlockSpec(memory_space=pltpu.HBM)
+    wide, tall = pu.shape[2], pd.shape[1]
+    outs = (
+        ((pu.shape[1], wide), bf16),
+        ((tall, pd.shape[2]), bf16),
+        ((pn.shape[1],), bf16),
+        ((pb.shape[1],), bf16),
+        *((x.shape, f32) for x in (mu, md, mn, mb)),
+        *((x.shape, f32) for x in (mu, md, mn, mb)),
+    )
+    rows, cols = mu.shape[0], md.shape[1]
+    results = pl.pallas_call(
+        exchange,
+        out_shape=[jax.ShapeDtypeStruct(shape, dtype) for shape, dtype in outs],
+        in_specs=[hbm, hbm, vmem, vmem, hbm, hbm, vmem, vmem, hbm, hbm, vmem, vmem],
+        out_specs=[vmem] * len(outs),
+        scratch_shapes=[
+            pltpu.VMEM(mu.shape, f32),
+            pltpu.VMEM(md.shape, f32),
+            pltpu.VMEM(mu.shape, f32),
+            pltpu.VMEM(md.shape, f32),
+            pltpu.VMEM(mu.shape, f32),
+            pltpu.VMEM(md.shape, f32),
+            pltpu.VMEM(mu.shape, f32),
+            pltpu.VMEM(md.shape, f32),
+            pltpu.VMEM((4, pn.shape[1]), f32),
+            pltpu.VMEM((4, pn.shape[1]), f32),
+            pltpu.VMEM((rows, lanes), f32),
+            pltpu.VMEM((8, cols), f32),
+            pltpu.VMEM((n, 2, rows), f32),
+            pltpu.VMEM((n, 2, cols), f32),
+            pltpu.SemaphoreType.DMA((6,)),
+            pltpu.SemaphoreType.DMA((2, chunks)),
+            pltpu.SemaphoreType.DMA((2, chunks)),
+            pltpu.SemaphoreType.DMA((2,)),
+            pltpu.SemaphoreType.DMA((2, n - 1)),
+            pltpu.SemaphoreType.DMA((2, n - 1)),
+            pltpu.SemaphoreType.DMA((2, 2)),
+            pltpu.SemaphoreType.DMA((2, 2)),
+        ],
+        compiler_params=pltpu.CompilerParams(
+            collective_id=0, has_side_effects=True, vmem_limit_bytes=40 * 2**20
+        ),
+        name="exchange",
+    )(*held((pu[0], pd[0])), pn, pb, *held((mu, md)), mn, mb, *held((eu, ed)), en, eb)
+    return tuple(pl.pallas_call(
+        place_results,
+        out_shape=[jax.ShapeDtypeStruct(shape, dtype) for shape, dtype in outs],
+        in_specs=[vmem] * len(outs),
+        out_specs=[hbm] * len(outs),
+        scratch_shapes=[pltpu.SemaphoreType.DMA((len(outs),))],
+        compiler_params=pltpu.CompilerParams(vmem_limit_bytes=2**20),
+        name="place_results",
+    )(*results))
+
+
 def solution(mesh):
     in_specs = (
         P(("job", "dp"), None, "tp"),
@@ -109,5 +433,5 @@
         P(("job", "dp")),
     )
     return jax.shard_map(
-        on_device, mesh=mesh, in_specs=in_specs, out_specs=out_specs, check_vma=False
-    )
+        on_device if mesh.shape["dp"] != 2 else on_pair, mesh=mesh, in_specs=in_specs, out_specs=out_specs, check_vma=False
+    )

time: 84.1 us -> 21.8 us (0.26)
  waiting for transfers between devices: 34.1 us -> 0 us
  blocking collectives: 18.3 us -> 0 us
  Pallas kernels: 0 us -> 16.7 us
  between operations: 13.9 us -> 0.67 us
  other arithmetic: 11.4 us -> 0 us
  local copies, waits for them, and re-layouts: 5.88 us -> 4.09 us
    reduce_scatter x2 -> x0, waiting for transfers between devices: 25 us -> none  [the longest x1 12.9 us: on_device(): lax.psum_scatter(partial_up[0], 'dp', scatter_dimension=0, tiled=True)]
    pallas_call x0 -> x2, Pallas kernels: none -> 16.7 us  [the longest x1 13.7 us: on_pair(): pl.pallas_call(exchange, out_shape=[jax.ShapeDtypeStruct(shape, dtype) fo...]
    psum x2 -> x0, blocking collectives: 14.7 us -> none  [the longest x1 12.2 us: on_device(): lax.psum((jnp.sum(master_up * master_up, axis=1, keepdims=True), jnp.sum(...]
    convert_element_type x4 -> x0, other arithmetic: 8.08 us -> none  [the longest x1 3.57 us: on_device(): stepped_down.astype(jnp.bfloat16)]
    all_gather x2 -> x0, waiting for transfers between devices: 7.73 us -> none  [the longest x1 7.73 us: on_device(): lax.all_gather(stepped_up.astype(jnp.bfloat16), 'dp', axis=0, tiled=True)]
    all_gather x2 -> x0, blocking collectives: 3.64 us -> none  [the longest x1 1.82 us: on_device(): lax.all_gather(stepped_norm.astype(jnp.bfloat16), 'dp', axis=0, tiled=True)]
    reduce_sum x4 -> x0, other arithmetic: 3.21 us -> none  [the longest x1 1.46 us: on_device(): jnp.sum(mean_up * mean_up, axis=1, keepdims=True)]
    unnamed x26 -> x12, local copies, waits for them, and re-layouts: 5.86 us -> 4.09 us
  transfers between devices with their start and end apart: 4 -> 0, of which waited for: 3 -> 0; matrix products, arithmetic and copies ran while one was open for 9% -> 0% of each run, Pallas kernels for 0% -> 0%
where the time goes in v1:
time: 21.8 us; the launch traced here: 21.5 us
  Pallas kernels  16.7 us (77%)
  local copies, waits for them, and re-layouts  4.09 us (19%)
  between operations  0.67 us (3%)
    pallas_call x1, Pallas kernels, on_pair(): pl.pallas_call(exchange, out_shape=[jax.ShapeDtypeStruct(shape, dtype) fo...  13.7 us
    unnamed x12, local copies, waits for them, and re-layouts  4.09 us
    pallas_call x1, Pallas kernels, on_pair(): pl.pallas_call(place_results, out_shape=[jax.ShapeDtypeStruct(shape, dtyp...  3.06 us

profile of v1, /device:TPU:0, one launch (start us, length us, event | category | flops | bytes accessed | tf_op | source)
XLA Modules:
  0.0 21.5 jit_solution(13345534844110155800)
XLA Ops:
  0.6 0.0 copy-start
  0.7 0.7 %copy-done = f32[1,768]{1,0:T(1,128)S(1)} copy-done((f32[1,768]{1,0:T(1,128)S(1)}, f32[1,768]{1,0:T(1,128)}, u32[]{:S(2)}) %copy-start) | copy-done | bytes 3096
  1.3 0.0 copy-start.1
  1.3 0.7 %copy-done.1 = f32[1,768]{1,0:T(1,128)S(1)} copy-done((f32[1,768]{1,0:T(1,128)S(1)}, f32[1,768]{1,0:T(1,128)}, u32[]{:S(2)}) %copy-start.1) | copy-done | bytes 3096
  2.0 0.0 copy-start.2
  2.0 0.7 %copy-done.2 = f32[384]{0:T(512)S(1)} copy-done((f32[384]{0:T(512)S(1)}, f32[384]{0:T(512)}, u32[]{:S(2)}) %copy-start.2) | copy-done | bytes 1560
  2.7 0.0 copy-start.3
  2.7 0.7 %copy-done.3 = f32[384]{0:T(512)S(1)} copy-done((f32[384]{0:T(512)S(1)}, f32[384]{0:T(512)}, u32[]{:S(2)}) %copy-start.3) | copy-done | bytes 1560
  3.4 0.0 copy-start.4
  3.4 0.7 %copy-done.4 = f32[384]{0:T(512)S(1)} copy-done((f32[384]{0:T(512)S(1)}, f32[384]{0:T(512)}, u32[]{:S(2)}) %copy-start.4) | copy-done | bytes 1560
  4.1 0.0 copy-start.5
  4.1 0.7 %copy-done.5 = f32[384]{0:T(512)S(1)} copy-done((f32[384]{0:T(512)S(1)}, f32[384]{0:T(512)}, u32[]{:S(2)}) %copy-start.5) | copy-done | bytes 1560
  4.7 13.7 %exchange.1 = (bf16[768,768]{1,0:T(8,128)(2,1)S(1)}, bf16[768,768]{1,0:T(8,128)(2,1)S(1)}, bf16[768]{0:T(1024)(128)(2,1)S(1)}, bf16[768]{0:T(1024)(128)(2,1)S(1)...) custom-call(f32[768,768]{1,0:T(8,128)} %bitcast.2, ...), custom_call_target="tpu_custom_call" | custom-call | tf_op jit(solution)/shard_map/exchange/pallas_call | solution.py:361
  18.4 3.1 %place_results.1 = (bf16[768,768]{1,0:T(8,128)(2,1)}, bf16[768,768]{1,0:T(8,128)(2,1)}, bf16[768]{0:T(1024)(128)(2,1)}, bf16[768]{0:T(1024)(128)(2,1)}, f32[384,...) custom-call(bf16[768,768]{1,0:T(8,128)(2,1)S(1)} %get-tuple-element., ...), custom_call_target="tpu_custom_call" | custom-call | tf_op jit(solution)/shard_map/place_results/pallas_call | solution.py:395
Async XLA Ops:
  0.6 0.7 %copy-start = (f32[1,768]{1,0:T(1,128)S(1)}, f32[1,768]{1,0:T(1,128)}, u32[]{:S(2)}) copy-start(f32[1,768]{1,0:T(1,128)} %pn.1) | copy-start | bytes 9220
  1.3 0.7 %copy-start.1 = (f32[1,768]{1,0:T(1,128)S(1)}, f32[1,768]{1,0:T(1,128)}, u32[]{:S(2)}) copy-start(f32[1,768]{1,0:T(1,128)} %pb.1) | copy-start | bytes 9220
  2.0 0.7 %copy-start.2 = (f32[384]{0:T(512)S(1)}, f32[384]{0:T(512)}, u32[]{:S(2)}) copy-start(f32[384]{0:T(512)} %mn.1) | copy-start | bytes 4612
  2.7 0.7 %copy-start.3 = (f32[384]{0:T(512)S(1)}, f32[384]{0:T(512)}, u32[]{:S(2)}) copy-start(f32[384]{0:T(512)} %mb.1) | copy-start | bytes 4612
  3.4 0.7 %copy-start.4 = (f32[384]{0:T(512)S(1)}, f32[384]{0:T(512)}, u32[]{:S(2)}) copy-start(f32[384]{0:T(512)} %en.1) | copy-start | bytes 4612
  4.1 0.7 %copy-start.5 = (f32[384]{0:T(512)S(1)}, f32[384]{0:T(512)}, u32[]{:S(2)}) copy-start(f32[384]{0:T(512)} %eb.1) | copy-start | bytes 4612

commit v2 on v1

--- a/solution.py
+++ b/solution.py
@@ -84,6 +84,7 @@
 
 
 chunks = 4
+pieces = 4
 lanes = 128
 
 
@@ -97,9 +98,9 @@
 def exchange(
     pu, pd, pn, pb, mu_h, md_h, mn, mb, eu_h, ed_h, en, eb,
     cu, cd, cn, cb, su, sd, sn, sb, tu, td, tn, tb,
-    own_u, own_d, got_u, got_d, mu, md, eu, ed, vec, got_vec,
+    own_u, own_d, give_u, give_d, got_u, got_d, mu, md, eu, ed, pn_v, pb_v, mn_v, mb_v, en_v, eb_v, vec, got_vec,
     sq_u, acc_d, stat_u, stat_d,
-    load_sem, part_send, part_recv, vec_sem, stat_send, stat_recv, out_send, out_recv,
+    load_sem, give_sem, knows, part_send, part_recv, vec_sem, stat_send, stat_recv, out_send, out_recv,
 ):
     me = lax.axis_index("dp")
     peer = 1 - me
@@ -116,11 +117,34 @@
     def theirs(size):
         return pl.ds(pl.multiple_of(peer * size, size), size)
 
+    has_left, has_right = here > 0, here < n - 1
+
+    def to_neighbours(left_sem, right_sem):
+        @pl.when(has_left)
+        def _():
+            pl.semaphore_signal(left_sem, inc=1, device_id={"tp": here - 1})
+
+        @pl.when(has_right)
+        def _():
+            pl.semaphore_signal(right_sem, inc=1, device_id={"tp": here + 1})
+
     barrier = pltpu.get_barrier_semaphore()
     pl.semaphore_signal(barrier, inc=1, device_id={"dp": peer})
-    for step in range(1, n):
-        pl.semaphore_signal(barrier, inc=1, device_id={"tp": lax.rem(here + step, n)})
-
+    to_neighbours(barrier, barrier)
+
+    give = []
+    for at in range(chunks):
+        span = pl.ds(at * part_u, part_u)
+        give.append(pltpu.make_async_copy(
+            pu.at[pl.ds(pl.multiple_of(peer * rows + at * part_u, 8), part_u), :],
+            give_u.at[span, :],
+            give_sem.at[0, at],
+        ))
+    for at in range(chunks):
+        span = pl.ds(at * part_d, part_d)
+        give.append(pltpu.make_async_copy(
+            pd.at[span, theirs(cols)], give_d.at[span, :], give_sem.at[1, at]
+        ))
     loads = [
         pltpu.make_async_copy(source, target, load_sem.at[at])
         for at, (source, target) in enumerate((
@@ -130,26 +154,24 @@
             (pd.at[:, mine(cols)], own_d),
             (eu_h, eu),
             (ed_h, ed),
+            (pn, pn_v),
+            (pb, pb_v),
+            (mn, mn_v),
+            (mb, mb_v),
+            (en, en_v),
+            (eb, eb_v),
         ))
     ]
-    for load in loads:
+    for load in give + loads[6:] + loads[:6]:
         load.start()
 
-    half = mn.shape[-1]
-    vec[0:1, :] = pn[...]
-    vec[1:2, :] = pb[...]
-    vec[2:3, :half] = mn[...].reshape(1, half)
-    vec[2:3, half:] = en[...].reshape(1, half)
-    vec[3:4, :half] = mb[...].reshape(1, half)
-    vec[3:4, half:] = eb[...].reshape(1, half)
-
-    pl.semaphore_wait(barrier, n)
+    pl.semaphore_wait(barrier, 1 + has_left.astype(jnp.int32) + has_right.astype(jnp.int32))
 
     send_u, send_d = [], []
     for at in range(chunks):
         span = pl.ds(at * part_u, part_u)
         send_u.append(pltpu.make_async_remote_copy(
-            src_ref=pu.at[pl.ds(pl.multiple_of(peer * rows + at * part_u, 8), part_u), :],
+            src_ref=give_u.at[span, :],
             dst_ref=got_u.at[span, :],
             send_sem=part_send.at[0, at],
             recv_sem=part_recv.at[0, at],
@@ -157,19 +179,27 @@
         ))
         span = pl.ds(at * part_d, part_d)
         send_d.append(pltpu.make_async_remote_copy(
-            src_ref=pd.at[span, theirs(cols)],
+            src_ref=give_d.at[span, :],
             dst_ref=got_d.at[span, :],
             send_sem=part_send.at[1, at],
             recv_sem=part_recv.at[1, at],
             device_id={"dp": peer},
         ))
-    for copy in send_u + send_d:
+    for load, copy in zip(give, send_u + send_d):
+        load.wait()
         copy.start()
-    send_vec = pltpu.make_async_remote_copy(
-        src_ref=vec, dst_ref=got_vec, send_sem=vec_sem.at[0], recv_sem=vec_sem.at[1],
-        device_id={"dp": peer},
-    )
-    send_vec.start()
+    if n > 2:
+        to_neighbours(knows.at[0], knows.at[1])
+
+    half = mn.shape[-1]
+    for load in loads[6:]:
+        load.wait()
+    vec[0:1, :] = pn_v[...]
+    vec[1:2, :] = pb_v[...]
+    vec[2:3, :half] = mn_v[...].reshape(1, half)
+    vec[2:3, half:] = en_v[...].reshape(1, half)
+    vec[3:4, :half] = mb_v[...].reshape(1, half)
+    vec[3:4, half:] = eb_v[...].reshape(1, half)
 
     step_u, step_d = 32, 64
 
@@ -190,11 +220,30 @@
             x = read(span)
             acc_d[...] += jnp.sum((x * x).reshape(step_d // 8, 8, cols), axis=0)
 
+    send_vec = pltpu.make_async_remote_copy(
+        src_ref=vec, dst_ref=got_vec, send_sem=vec_sem.at[0], recv_sem=vec_sem.at[1],
+        device_id={"dp": peer},
+    )
+    send_vec.start()
+
+    def hear():
+        @pl.when(has_right)
+        def _():
+            pl.semaphore_wait(knows.at[0], 1)
+
+        @pl.when(has_left)
+        def _():
+            pl.semaphore_wait(knows.at[1], 1)
+
     loads[1].wait()
     acc_d[...] = jnp.zeros_like(acc_d)
     down_squares(lambda span: md[span, :], 0, tall)
     stat_d[pl.ds(here, 1), 0:1, :] = jnp.sum(acc_d[...], axis=0).reshape(1, 1, cols)
     acc_d[...] = jnp.zeros_like(acc_d)
+    for reach in range(2, n):
+        hear()
+        if reach < n - 1:
+            to_neighbours(knows.at[0], knows.at[1])
 
     def to_peers(stat, which):
         copies = []
@@ -265,7 +314,6 @@
     sq_u[...] = jnp.broadcast_to(ratio_of(stat_u), (lanes, rows)).T
 
     out = []
-    pieces = 2
     for piece in range(pieces):
         size = rows // pieces
 
@@ -329,9 +377,18 @@
 def place_results(*refs):
     count = (len(refs) - 1) // 2
     sem = refs[-1]
-    copies = [
-        pltpu.make_async_copy(refs[at], refs[count + at], sem.at[at]) for at in range(count)
-    ]
+    copies = []
+    for at in range(count):
+        source, target = refs[at], refs[count + at]
+        if len(source.shape) == 1:
+            copies.append(pltpu.make_async_copy(source, target, sem.at[at, 0]))
+            continue
+        size = source.shape[0] // pieces
+        for piece in range(pieces):
+            span = pl.ds(piece * size, size)
+            copies.append(pltpu.make_async_copy(
+                source.at[span, :], target.at[span, :], sem.at[at, piece]
+            ))
     for copy in copies:
         copy.start()
     for copy in copies:
@@ -361,43 +418,39 @@
     results = pl.pallas_call(
         exchange,
         out_shape=[jax.ShapeDtypeStruct(shape, dtype) for shape, dtype in outs],
-        in_specs=[hbm, hbm, vmem, vmem, hbm, hbm, vmem, vmem, hbm, hbm, vmem, vmem],
+        in_specs=[hbm] * len(args),
         out_specs=[vmem] * len(outs),
         scratch_shapes=[
-            pltpu.VMEM(mu.shape, f32),
-            pltpu.VMEM(md.shape, f32),
-            pltpu.VMEM(mu.shape, f32),
-            pltpu.VMEM(md.shape, f32),
-            pltpu.VMEM(mu.shape, f32),
-            pltpu.VMEM(md.shape, f32),
-            pltpu.VMEM(mu.shape, f32),
-            pltpu.VMEM(md.shape, f32),
+            *(pltpu.VMEM(x.shape, f32) for x in (mu, md) * 5),
+            *(pltpu.VMEM(x.shape, f32) for x in (pn, pb, mn, mb, en, eb)),
             pltpu.VMEM((4, pn.shape[1]), f32),
             pltpu.VMEM((4, pn.shape[1]), f32),
             pltpu.VMEM((rows, lanes), f32),
             pltpu.VMEM((8, cols), f32),
             pltpu.VMEM((n, 2, rows), f32),
             pltpu.VMEM((n, 2, cols), f32),
-            pltpu.SemaphoreType.DMA((6,)),
+            pltpu.SemaphoreType.DMA((12,)),
+            pltpu.SemaphoreType.DMA((2, chunks)),
+            pltpu.SemaphoreType.REGULAR((2,)),
             pltpu.SemaphoreType.DMA((2, chunks)),
             pltpu.SemaphoreType.DMA((2, chunks)),
             pltpu.SemaphoreType.DMA((2,)),
             pltpu.SemaphoreType.DMA((2, n - 1)),
             pltpu.SemaphoreType.DMA((2, n - 1)),
-            pltpu.SemaphoreType.DMA((2, 2)),
-            pltpu.SemaphoreType.DMA((2, 2)),
+            pltpu.SemaphoreType.DMA((2, pieces)),
+            pltpu.SemaphoreType.DMA((2, pieces)),
         ],
         compiler_params=pltpu.CompilerParams(
             collective_id=0, has_side_effects=True, vmem_limit_bytes=40 * 2**20
         ),
         name="exchange",
-    )(*held((pu[0], pd[0])), pn, pb, *held((mu, md)), mn, mb, *held((eu, ed)), en, eb)
+    )(*held((pu[0], pd[0], *args[2:])))
     return tuple(pl.pallas_call(
         place_results,
         out_shape=[jax.ShapeDtypeStruct(shape, dtype) for shape, dtype in outs],
         in_specs=[vmem] * len(outs),
         out_specs=[hbm] * len(outs),
-        scratch_shapes=[pltpu.SemaphoreType.DMA((len(outs),))],
+        scratch_shapes=[pltpu.SemaphoreType.DMA((len(outs), pieces))],
         compiler_params=pltpu.CompilerParams(vmem_limit_bytes=2**20),
         name="place_results",
     )(*results))

time: 21.8 us -> 20 us (0.917)
  local copies, waits for them, and re-layouts: 4.09 us -> 0 us
  Pallas kernels: 16.7 us -> 19.2 us
    unnamed x12 -> x0, local copies, waits for them, and re-layouts: 4.09 us -> none
    pallas_call x1, Pallas kernels: 13.7 us -> 15.9 us  [on_pair(): pl.pallas_call(exchange, out_shape=[jax.ShapeDtypeStruct(shape, dtype) fo...]
    pallas_call x1, Pallas kernels: 3.06 us -> 3.34 us  [on_pair(): pl.pallas_call(place_results, out_shape=[jax.ShapeDtypeStruct(shape, dtyp...]
where the time goes in v2:
time: 20 us; the launch traced here: 19.9 us
  Pallas kernels  19.2 us (96%)
  between operations  0.66 us (3%)
    pallas_call x1, Pallas kernels, on_pair(): pl.pallas_call(exchange, out_shape=[jax.ShapeDtypeStruct(shape, dtype) fo...  15.9 us
    pallas_call x1, Pallas kernels, on_pair(): pl.pallas_call(place_results, out_shape=[jax.ShapeDtypeStruct(shape, dtyp...  3.34 us

profile of v2, /device:TPU:0, one launch (start us, length us, event | category | flops | bytes accessed | tf_op | source)
XLA Modules:
  0.0 19.9 jit_solution(14994484295136466263)
XLA Ops:
  0.6 15.9 %exchange.1 = (bf16[768,768]{1,0:T(8,128)(2,1)S(1)}, bf16[768,768]{1,0:T(8,128)(2,1)S(1)}, bf16[768]{0:T(1024)(128)(2,1)S(1)}, bf16[768]{0:T(1024)(128)(2,1)S(1)...) custom-call(f32[768,768]{1,0:T(8,128)} %bitcast.2, ...), custom_call_target="tpu_custom_call" | custom-call | tf_op jit(solution)/shard_map/exchange/pallas_call | solution.py:418
  16.5 3.3 %place_results.1 = (bf16[768,768]{1,0:T(8,128)(2,1)}, bf16[768,768]{1,0:T(8,128)(2,1)}, bf16[768]{0:T(1024)(128)(2,1)}, bf16[768]{0:T(1024)(128)(2,1)}, f32[384,...) custom-call(bf16[768,768]{1,0:T(8,128)(2,1)S(1)} %get-tuple-element., ...), custom_call_target="tpu_custom_call" | custom-call | tf_op jit(solution)/shard_map/place_results/pallas_call | solution.py:448

commit v3 on v2

--- a/solution.py
+++ b/solution.py
@@ -100,7 +100,7 @@
     cu, cd, cn, cb, su, sd, sn, sb, tu, td, tn, tb,
     own_u, own_d, give_u, give_d, got_u, got_d, mu, md, eu, ed, pn_v, pb_v, mn_v, mb_v, en_v, eb_v, vec, got_vec,
     sq_u, acc_d, stat_u, stat_d,
-    load_sem, give_sem, knows, part_send, part_recv, vec_sem, stat_send, stat_recv, out_send, out_recv,
+    load_sem, give_sem, part_send, part_recv, vec_sem, stat_send, stat_recv, out_send, out_recv,
 ):
     me = lax.axis_index("dp")
     peer = 1 - me
@@ -117,20 +117,10 @@
     def theirs(size):
         return pl.ds(pl.multiple_of(peer * size, size), size)
 
-    has_left, has_right = here > 0, here < n - 1
-
-    def to_neighbours(left_sem, right_sem):
-        @pl.when(has_left)
-        def _():
-            pl.semaphore_signal(left_sem, inc=1, device_id={"tp": here - 1})
-
-        @pl.when(has_right)
-        def _():
-            pl.semaphore_signal(right_sem, inc=1, device_id={"tp": here + 1})
-
     barrier = pltpu.get_barrier_semaphore()
     pl.semaphore_signal(barrier, inc=1, device_id={"dp": peer})
-    to_neighbours(barrier, barrier)
+    for step in range(1, n):
+        pl.semaphore_signal(barrier, inc=1, device_id={"tp": lax.rem(here + step, n)})
 
     give = []
     for at in range(chunks):
@@ -162,16 +152,14 @@
             (eb, eb_v),
         ))
     ]
-    for load in give + loads[6:] + loads[:6]:
-        load.start()
-
-    pl.semaphore_wait(barrier, 1 + has_left.astype(jnp.int32) + has_right.astype(jnp.int32))
+
+    pl.semaphore_wait(barrier, n)
 
     send_u, send_d = [], []
     for at in range(chunks):
         span = pl.ds(at * part_u, part_u)
         send_u.append(pltpu.make_async_remote_copy(
-            src_ref=give_u.at[span, :],
+            src_ref=pu.at[pl.ds(pl.multiple_of(peer * rows + at * part_u, 8), part_u), :],
             dst_ref=got_u.at[span, :],
             send_sem=part_send.at[0, at],
             recv_sem=part_recv.at[0, at],
@@ -179,17 +167,20 @@
         ))
         span = pl.ds(at * part_d, part_d)
         send_d.append(pltpu.make_async_remote_copy(
-            src_ref=give_d.at[span, :],
+            src_ref=pd.at[span, theirs(cols)],
             dst_ref=got_d.at[span, :],
             send_sem=part_send.at[1, at],
             recv_sem=part_recv.at[1, at],
             device_id={"dp": peer},
         ))
-    for load, copy in zip(give, send_u + send_d):
-        load.wait()
+    for load, copy in zip(give[:chunks], send_u):
         copy.start()
-    if n > 2:
-        to_neighbours(knows.at[0], knows.at[1])
+    for load in (loads[0], loads[2], *loads[6:]):
+        load.start()
+    for load, copy in zip(give[chunks:], send_d):
+        copy.start()
+    for load in (loads[1], *loads[3:6]):
+        load.start()
 
     half = mn.shape[-1]
     for load in loads[6:]:
@@ -226,24 +217,11 @@
     )
     send_vec.start()
 
-    def hear():
-        @pl.when(has_right)
-        def _():
-            pl.semaphore_wait(knows.at[0], 1)
-
-        @pl.when(has_left)
-        def _():
-            pl.semaphore_wait(knows.at[1], 1)
-
     loads[1].wait()
     acc_d[...] = jnp.zeros_like(acc_d)
     down_squares(lambda span: md[span, :], 0, tall)
     stat_d[pl.ds(here, 1), 0:1, :] = jnp.sum(acc_d[...], axis=0).reshape(1, 1, cols)
     acc_d[...] = jnp.zeros_like(acc_d)
-    for reach in range(2, n):
-        hear()
-        if reach < n - 1:
-            to_neighbours(knows.at[0], knows.at[1])
 
     def to_peers(stat, which):
         copies = []
@@ -377,18 +355,9 @@
 def place_results(*refs):
     count = (len(refs) - 1) // 2
     sem = refs[-1]
-    copies = []
-    for at in range(count):
-        source, target = refs[at], refs[count + at]
-        if len(source.shape) == 1:
-            copies.append(pltpu.make_async_copy(source, target, sem.at[at, 0]))
-            continue
-        size = source.shape[0] // pieces
-        for piece in range(pieces):
-            span = pl.ds(piece * size, size)
-            copies.append(pltpu.make_async_copy(
-                source.at[span, :], target.at[span, :], sem.at[at, piece]
-            ))
+    copies = [
+        pltpu.make_async_copy(refs[at], refs[count + at], sem.at[at]) for at in range(count)
+    ]
     for copy in copies:
         copy.start()
     for copy in copies:
@@ -431,7 +400,6 @@
             pltpu.VMEM((n, 2, cols), f32),
             pltpu.SemaphoreType.DMA((12,)),
             pltpu.SemaphoreType.DMA((2, chunks)),
-            pltpu.SemaphoreType.REGULAR((2,)),
             pltpu.SemaphoreType.DMA((2, chunks)),
             pltpu.SemaphoreType.DMA((2, chunks)),
             pltpu.SemaphoreType.DMA((2,)),
@@ -450,7 +418,7 @@
         out_shape=[jax.ShapeDtypeStruct(shape, dtype) for shape, dtype in outs],
         in_specs=[vmem] * len(outs),
         out_specs=[hbm] * len(outs),
-        scratch_shapes=[pltpu.SemaphoreType.DMA((len(outs), pieces))],
+        scratch_shapes=[pltpu.SemaphoreType.DMA((len(outs),))],
         compiler_params=pltpu.CompilerParams(vmem_limit_bytes=2**20),
         name="place_results",
     )(*results))

time: 20 us -> 17.7 us (0.89)
  Pallas kernels: 19.2 us -> 16.9 us
    pallas_call x1, Pallas kernels: 15.9 us -> 13.8 us  [on_pair(): pl.pallas_call(exchange, out_shape=[jax.ShapeDtypeStruct(shape, dtype) fo...]
    pallas_call x1, Pallas kernels: 3.34 us -> 3.06 us  [on_pair(): pl.pallas_call(place_results, out_shape=[jax.ShapeDtypeStruct(shape, dtyp...]
where the time goes in v3:
time: 17.7 us; the launch traced here: 17.6 us
  Pallas kernels  16.9 us (95%)
  between operations  0.66 us (4%)
    pallas_call x1, Pallas kernels, on_pair(): pl.pallas_call(exchange, out_shape=[jax.ShapeDtypeStruct(shape, dtype) fo...  13.8 us
    pallas_call x1, Pallas kernels, on_pair(): pl.pallas_call(place_results, out_shape=[jax.ShapeDtypeStruct(shape, dtyp...  3.06 us

profile of v3, /device:TPU:0, one launch (start us, length us, event | category | flops | bytes accessed | tf_op | source)
XLA Modules:
  0.0 17.6 jit_solution(3983953278076039597)
XLA Ops:
  0.6 13.8 %exchange.1 = (bf16[768,768]{1,0:T(8,128)(2,1)S(1)}, bf16[768,768]{1,0:T(8,128)(2,1)S(1)}, bf16[768]{0:T(1024)(128)(2,1)S(1)}, bf16[768]{0:T(1024)(128)(2,1)S(1)...) custom-call(f32[768,768]{1,0:T(8,128)} %bitcast.2, ...), custom_call_target="tpu_custom_call" | custom-call | tf_op jit(solution)/shard_map/exchange/pallas_call | solution.py:387
  14.5 3.1 %place_results.1 = (bf16[768,768]{1,0:T(8,128)(2,1)}, bf16[768,768]{1,0:T(8,128)(2,1)}, bf16[768]{0:T(1024)(128)(2,1)}, bf16[768]{0:T(1024)(128)(2,1)}, f32[384,...) custom-call(bf16[768,768]{1,0:T(8,128)(2,1)S(1)} %get-tuple-element., ...), custom_call_target="tpu_custom_call" | custom-call | tf_op jit(solution)/shard_map/place_results/pallas_call | solution.py:416

commit v4 on v3

--- a/solution.py
+++ b/solution.py
@@ -179,7 +179,7 @@
         load.start()
     for load, copy in zip(give[chunks:], send_d):
         copy.start()
-    for load in (loads[1], *loads[3:6]):
+    for load in (loads[1], loads[3]):
         load.start()
 
     half = mn.shape[-1]
@@ -250,6 +250,8 @@
 
     stat_u[pl.ds(here, 1), 1:2, :] = jnp.sum(sq_u[...].T, axis=0).reshape(1, 1, rows)
     stats_u = to_peers(stat_u, 0)
+    for load in loads[4:6]:
+        load.start()
 
     loads[3].wait()
 

time: 17.7 us -> 17.7 us (level)
  no operation moved by 1% of the time
where the time goes in v4:
time: 17.7 us; the launch traced here: 17.6 us
  Pallas kernels  16.9 us (95%)
  between operations  0.66 us (4%)
    pallas_call x1, Pallas kernels, on_pair(): pl.pallas_call(exchange, out_shape=[jax.ShapeDtypeStruct(shape, dtype) fo...  13.8 us
    pallas_call x1, Pallas kernels, on_pair(): pl.pallas_call(place_results, out_shape=[jax.ShapeDtypeStruct(shape, dtyp...  3.06 us

profile of v4, /device:TPU:0, one launch (start us, length us, event | category | flops | bytes accessed | tf_op | source)
XLA Modules:
  0.0 17.6 jit_solution(1948472774089945861)
XLA Ops:
  0.6 13.8 %exchange.1 = (bf16[768,768]{1,0:T(8,128)(2,1)S(1)}, bf16[768,768]{1,0:T(8,128)(2,1)S(1)}, bf16[768]{0:T(1024)(128)(2,1)S(1)}, bf16[768]{0:T(1024)(128)(2,1)S(1)...) custom-call(f32[768,768]{1,0:T(8,128)} %bitcast.2, ...), custom_call_target="tpu_custom_call" | custom-call | tf_op jit(solution)/shard_map/exchange/pallas_call | solution.py:389
  14.5 3.1 %place_results.1 = (bf16[768,768]{1,0:T(8,128)(2,1)}, bf16[768,768]{1,0:T(8,128)(2,1)}, bf16[768]{0:T(1024)(128)(2,1)}, bf16[768]{0:T(1024)(128)(2,1)}, f32[384,...) custom-call(bf16[768,768]{1,0:T(8,128)(2,1)S(1)} %get-tuple-element., ...), custom_call_target="tpu_custom_call" | custom-call | tf_op jit(solution)/shard_map/place_results/pallas_call | solution.py:418
